TPU v7x, 16 devices: a whole 2x2x2 slice. The times are simulated.
16 devices in a mesh: rep: 1, r: 4 (over y, z), s: 4 (over x, core).
Axes of the slice: x: 2, y: 2, z: 2, core: 2. Of those that a mesh axis runs over, the one named last changes fastest.
Arguments:
- x: bfloat16 [16, 4096, 1024], P(('rep', 'r', 's'))
- dy: bfloat16 [16, 4096, 1024], P(('rep', 'r', 's'))
- w_gate: bfloat16 [2, 1024, 4096], P(None, 's')
- w_up: bfloat16 [2, 1024, 4096], P(None, 's')
- w_down: bfloat16 [2, 4096, 1024], P(None, 's')
Outputs:
- output 1: bfloat16 [16, 4096, 1024], P(('rep', 'r', 's'))
- output 2: bfloat16 [2, 1024, 4096], P('rep', 's')
- output 3: bfloat16 [2, 1024, 4096], P('rep', 's')
- output 4: bfloat16 [2, 4096, 1024], P('rep', 's')
All inputs are finite; a program needn't handle non-finite values.
Results may differ from a plain program's by a relative error of at most 0.018.
Values are sent between devices in bfloat16 or wider.
A program may use at most 2 GiB of HBM per device.

v0:
```python
import jax
import jax.numpy as jnp
from jax import lax
from jax.sharding import PartitionSpec as P

NAMES = ("w_gate", "w_up", "w_down")


def matmul(a, w):
    return jnp.dot(a, w, preferred_element_type=jnp.float32).astype(jnp.bfloat16)


def normed(h):
    wide = h.astype(jnp.float32)
    scale = lax.rsqrt(jnp.mean(wide**2, -1, keepdims=True) + 1e-6)
    return (wide * scale).astype(jnp.bfloat16)


def layer(h, w):
    a = normed(h)
    gate = jnp.dot(a, w["w_gate"], preferred_element_type=jnp.float32)
    up = jnp.dot(a, w["w_up"], preferred_element_type=jnp.float32)
    return h + matmul((jax.nn.silu(gate) * up).astype(jnp.bfloat16), w["w_down"])


def solution(mesh):
    def fetched(weights, number):
        return {name: lax.all_gather(w[number], "s", axis=0, tiled=True) for name, w in zip(NAMES, weights, strict=True)}

    def summed(term):
        return lax.psum(lax.psum_scatter(term, "s", scatter_dimension=0, tiled=True), "r")

    def step(x, dy, *weights):
        layers = weights[0].shape[0]
        h, inputs = x[0], []
        for number in range(layers):
            inputs.append(h)
            h = layer(h, fetched(weights, number))
        by_h, mine = dy[0], [None] * layers
        for number in reversed(range(layers)):
            _, back = jax.vjp(lambda w, h: layer(h, w), fetched(weights, number), inputs[number])
            by_w, by_h = back(by_h)
            mine[number] = [summed(by_w[name]) for name in NAMES]
        return (by_h[None], *(jnp.stack([mine[number][i] for number in range(layers)]) for i in range(3)))

    states, cut = P(("rep", "r", "s"), None, None), P(None, "s", None)
    return jax.shard_map(
        step,
        mesh=mesh,
        in_specs=(states, states) + (cut,) * 3,
        out_specs=(states,) + (P("rep", "s", None),) * 3,
        check_vma=False,
    )
```

profile of v0, /device:TPU:0, one launch (start us, length us, event | category | flops | bytes accessed | tf_op | source)
XLA Modules:
  0.0 1311.1 jit_solution(14143408104765340289)
XLA Ops:
  7.2 0.0 all-gather.13.cloned.1.call-start
  7.2 4.7 fusion.72
  11.9 0.0 all-gather.13.cloned.1.call-update
  12.0 0.0 all-gather.15.cloned.1.call-start
  12.0 4.7 fusion.71
  16.7 0.0 all-gather.15.cloned.1.call-update
  16.8 0.0 all-gather.17.cloned.1.call-start
  16.8 4.7 fusion.70
  21.5 0.0 all-gather.17.cloned.1.call-update
  21.5 0.0 all-gather.23.cloned.1.call-start
  21.6 0.5 all-gather.23.cloned.1.call-update
  22.1 0.0 all-gather.21.cloned.1.call-start
  22.1 0.5 all-gather.21.cloned.1.call-update
  22.7 0.0 all-gather.19.cloned.1.call-start
  22.7 0.5 all-gather.19.cloned.1.call-update
  23.3 0.0 reduce-scatter.15.cloned.1.call-start
  23.3 11.9 copy.10
  35.2 5.1 fusion.15
  40.3 0.6 copy-done
  40.9 11.4 copy.9
  52.4 19.2 %all-gather.13.cloned.1.call-done = bf16[1,1024,4096]{2,1,0:T(8,128)(2,1)} async-done(((bf16[1,256,4096]{2,1,0:T(8,128)(2,1)}), bf16[1,1024,4096]{2,1,0:T(8,128)(2,1)}) %all-gather.13.cloned.1.call-update) | async-done | bytes 8388624 | tf_op jit(solution)/shard_map/all_gather | solution.py:28
  71.6 45.6 %fusion.42 = f32[4096,4096]{1,0:T(8,128)} fusion(bf16[1,1024,4096]{2,1,0:T(8,128)(2,1)} %all-gather.13.cloned.1.call-done, bf16[1,4096,1024]{1,2,0:T(8,128)(2,1)} %copy.10, f32[4096]{0:T(1024)S(1)} %fusion.63), kind=kOutput, calls=%fused_computation.64 | convolution fusion | flops 34372321280 | bytes 83902464 | tf_op jit(solution)/shard_map/dot_general | solution.py:21
  117.2 12.6 all-gather.15.cloned.1.call-done
  129.8 72.7 %multiply_convert_fusion.1 = (bf16[4096,4096]{1,0:T(8,128)(2,1)}, f32[4096,4096]{1,0:T(8,128)}) fusion(f32[4096,4096]{1,0:T(8,128)} %fusion.42, bf16[1,1024,4096]{2,1,0:T(8,128)(2,1)} %all-gather.15.cloned.1.call-done, bf16[1,4096,1024]{1,2,0:T(8,128)(2,1)} %copy.10, f32[4096]{0:T(1024)S(1)} %fusion.63), kind=kOutput, calls=%fused_computation.13 | convolution fusion | flops 34472984576 | bytes 184565760 | tf_op jit(solution)/shard_map/dot_general | solution.py:22
  202.5 43.1 %fusion.18 = (f32[4096]{0:T(1024)S(1)}, bf16[4096,1024]{0,1:T(8,128)(2,1)}) fusion(bf16[4096,4096]{1,0:T(8,128)(2,1)} %get-tuple-element.20, bf16[1,4096,1024]{2,1,0:T(8,128)(2,1)} %all-gather.17.cloned.1.call-done, bf16[1,4096,1024]{1,2,0:T(8,128)(2,1)} %copy.10), kind=kOutput, calls=%fused_computation.40 | convolution fusion | flops 34380705792 | bytes 58736640 | tf_op jit(solution)/shard_map/dot_general | solution.py:10
  245.7 0.6 copy-done.9
  246.3 0.3 all-gather.23.cloned.1.call-done
  246.6 46.0 %fusion.26 = f32[4096,4096]{1,0:T(8,128)} fusion(bf16[1,1024,4096]{2,1,0:T(8,128)(2,1)} %all-gather.23.cloned.1.call-done, bf16[4096,1024]{0,1:T(8,128)(2,1)} %get-tuple-element.23, f32[4096]{0:T(1024)S(1)} %fusion.64), kind=kOutput, calls=%fused_computation.48 | convolution fusion | flops 34372321280 | bytes 83902464 | tf_op jit(solution)/shard_map/jvp()/dot_general | solution.py:22
  292.6 12.0 all-gather.21.cloned.1.call-done
  304.7 43.3 %convolution_convert_fusion.1 = bf16[4096,4096]{1,0:T(8,128)(2,1)} fusion(bf16[1,4096,1024]{2,1,0:T(8,128)(2,1)} %param.6, bf16[1,4096,1024]{2,1,0:T(8,128)(2,1)} %all-gather.21.cloned.1.call-done), kind=kOutput, calls=%fused_computation.22 | convolution fusion | flops 34376515584 | bytes 50331648 | tf_op jit(solution)/shard_map/transpose(jvp())/dot_general | solution.py:10
  348.0 15.3 %all-gather.19.cloned.1.call-done = bf16[1,1024,4096]{2,1,0:T(8,128)(2,1)} async-done(((bf16[1,256,4096]{2,1,0:T(8,128)(2,1)}), bf16[1,1024,4096]{2,1,0:T(8,128)(2,1)}) %all-gather.19.cloned.1.call-update) | async-done | bytes 8388624 | tf_op jit(solution)/shard_map/all_gather | solution.py:28
  363.3 83.9 %fusion.1 = (bf16[4096,4096]{1,0:T(8,128)(2,1)}, f32[4096,4096]{1,0:T(8,128)}) fusion(f32[4096,4096]{1,0:T(8,128)} %fusion.26, bf16[4096,4096]{1,0:T(8,128)(2,1)} %convolution_convert_fusion.1, bf16[1,1024,4096]{2,1,0:T(8,128)(2,1)} %all-gather.19.cloned.1.call-done, bf16[4096,1024]{0,1:T(8,128)(2,1)} %get-tuple-element.23, f32[4096]{0:T(1024)S(1)} %fusion.64), kind=kOutput, calls=%fused_computation.7 | convolution fusion | flops 34573647872 | bytes 218120192 | tf_op jit(solution)/shard_map/jvp()/dot_general | solution.py:21
  447.2 43.0 %fusion.30 = bf16[4096,1024]{0,1:T(8,128)(2,1)} fusion(bf16[4096,4096]{1,0:T(8,128)(2,1)} %get-tuple-element.24, bf16[1,1024,4096]{2,1,0:T(8,128)(2,1)} %all-gather.19.cloned.1.call-done), kind=kOutput, calls=%fused_computation.52 | convolution fusion | flops 34359738368 | bytes 50331648 | tf_op jit(solution)/shard_map/transpose(jvp())/dot_general | solution.py:21
  490.2 52.8 %fusion.20 = (f32[4096]{0:T(1024)S(1)}, bf16[4096,1024]{0,1:T(8,128)(2,1)}) fusion(bf16[4096,1024]{0,1:T(8,128)(2,1)} %get-tuple-element.23, bf16[4096,1024]{0,1:T(8,128)(2,1)} %fusion.30, bf16[1,1024,4096]{2,1,0:T(8,128)(2,1)} %all-gather.23.cloned.1.call-done, bf16[4096,4096]{1,0:T(8,128)(2,1)} %convolution_convert_fusion.1, ...), kind=kOutput, calls=%fused_computation.42 | convolution fusion | flops 34485563392 | bytes 134234112 | tf_op jit(solution)/shard_map/transpose(jvp())/dot_general | solution.py:22
  543.1 14.0 %fusion.23 = bf16[4096,1024]{0,1:T(8,128)(2,1)} fusion(bf16[4096,1024]{0,1:T(8,128)(2,1)} %get-tuple-element.23, bf16[4096,1024]{0,1:T(8,128)(2,1)} %get-tuple-element.27, bf16[1,4096,1024]{1,2,0:T(8,128)(2,1)} %copy.9, f32[4096]{0:T(1024)S(1)} %multiply_multiply_fusion.1, f32[4096]{0:T(1024)S(1)} %copy-done.7), kind=kLoop, calls=%fused_computation.45 | loop fusion | flops 29360128 | bytes 33587200 | tf_op jit(solution)/shard_map/transpose(jvp())/add_any | solution.py:14
  557.1 42.7 %convolution_convert_fusion.4 = bf16[4096,1024]{1,0:T(8,128)(2,1)} fusion(bf16[4096,4096]{1,0:T(8,128)(2,1)} %get-tuple-element.20, bf16[4096,1024]{0,1:T(8,128)(2,1)} %fusion.23), kind=kOutput, calls=%fused_computation.74 | convolution fusion | flops 34363932672 | bytes 50331648 | tf_op jit(solution)/shard_map/transpose(jvp())/dot_general | solution.py:10
  599.7 0.0 reduce-scatter.15.cloned.1.call-update
  599.7 0.0 reduce-scatter.17.cloned.1.call-start
  599.8 52.6 %fusion.46 = bf16[4096,1024]{1,0:T(8,128)(2,1)} fusion(bf16[1,4096,1024]{2,1,0:T(8,128)(2,1)} %param.6, f32[4096,4096]{1,0:T(8,128)} %fusion.26, f32[4096,4096]{1,0:T(8,128)} %get-tuple-element.25), kind=kOutput, calls=%fused_computation.69 | convolution fusion | flops 34464595968 | bytes 150994944 | tf_op jit(solution)/shard_map/transpose(jvp())/dot_general | solution.py:10
  652.4 0.0 reduce-scatter.17.cloned.1.call-update
  652.5 0.0 reduce-scatter.11.cloned.1.call-start
  652.5 83.1 %fusion.3 = (bf16[4096,4096]{1,0:T(8,128)(2,1)}, bf16[4096,4096]{1,0:T(8,128)(2,1)}) fusion(f32[4096,4096]{1,0:T(8,128)} %fusion.42, f32[4096,4096]{1,0:T(8,128)} %get-tuple-element.21, bf16[4096,1024]{0,1:T(8,128)(2,1)} %fusion.23, bf16[1,4096,1024]{2,1,0:T(8,128)(2,1)} %all-gather.17.cloned.1.call-done), kind=kOutput, calls=%fused_computation.9 | convolution fusion | flops 34577842176 | bytes 218103808 | tf_op jit(solution)/shard_map/transpose(jvp())/dot_general | solution.py:10
  735.6 46.5 %fusion.53 = bf16[1024,4096]{1,0:T(8,128)(2,1)} fusion(bf16[4096,4096]{1,0:T(8,128)(2,1)} %get-tuple-element.29, bf16[1,4096,1024]{1,2,0:T(8,128)(2,1)} %copy.10, f32[4096]{0:T(1024)S(1)} %copy-done.3, f32[4096,4096]{1,0:T(8,128)} %fusion.42), kind=kOutput, calls=%fused_computation.72 | convolution fusion | flops 34477178880 | bytes 117456896 | tf_op jit(solution)/shard_map/transpose(jvp())/dot_general | solution.py:22
  782.0 0.0 reduce-scatter.11.cloned.1.call-update
  782.1 0.0 reduce-scatter.13.cloned.1.call-start
  782.1 46.6 %fusion.54 = bf16[1024,4096]{1,0:T(8,128)(2,1)} fusion(bf16[4096,4096]{1,0:T(8,128)(2,1)} %convolution_convert_fusion.1, bf16[4096,1024]{0,1:T(8,128)(2,1)} %get-tuple-element.23, f32[4096]{0:T(1024)S(1)} %copy-done.8, f32[4096,4096]{1,0:T(8,128)} %get-tuple-element.25), kind=kOutput, calls=%fused_computation.73 | convolution fusion | flops 34477178880 | bytes 117456896 | tf_op jit(solution)/shard_map/transpose(jvp())/dot_general | solution.py:22
  828.7 0.0 reduce-scatter.13.cloned.1.call-update
  828.8 0.0 reduce-scatter.9.cloned.1.call-start
  828.8 42.5 %convolution_convert_fusion.2 = bf16[1024,4096]{1,0:T(8,128)(2,1)} fusion(bf16[4096,4096]{1,0:T(8,128)(2,1)} %get-tuple-element.24, bf16[4096,1024]{0,1:T(8,128)(2,1)} %get-tuple-element.23, f32[4096]{0:T(1024)S(1)} %copy-done.8), kind=kOutput, calls=%fused_computation.70 | convolution fusion | flops 34372321280 | bytes 50348032 | tf_op jit(solution)/shard_map/transpose(jvp())/dot_general | solution.py:21
  871.3 0.0 reduce-scatter.7.cloned.1.call-start
  871.4 42.5 %convolution_convert_fusion.3 = bf16[1024,4096]{1,0:T(8,128)(2,1)} fusion(bf16[4096,4096]{1,0:T(8,128)(2,1)} %get-tuple-element.28, bf16[1,4096,1024]{1,2,0:T(8,128)(2,1)} %copy.10, f32[4096]{0:T(1024)S(1)} %copy-done.4), kind=kOutput, calls=%fused_computation.71 | convolution fusion | flops 34372321280 | bytes 50348032 | tf_op jit(solution)/shard_map/transpose(jvp())/dot_general | solution.py:21
  913.9 0.0 reduce-scatter.7.cloned.1.call-update
  913.9 0.0 all-reduce.3.cloned.1.call-start
  913.9 42.9 %fusion.40 = bf16[4096,1024]{0,1:T(8,128)(2,1)} fusion(bf16[4096,4096]{1,0:T(8,128)(2,1)} %get-tuple-element.28, bf16[1,1024,4096]{2,1,0:T(8,128)(2,1)} %all-gather.13.cloned.1.call-done), kind=kOutput, calls=%fused_computation.62 | convolution fusion | flops 34359738368 | bytes 50331648 | tf_op jit(solution)/shard_map/transpose(jvp())/dot_general | solution.py:21
  956.8 0.0 reduce-scatter.13.cloned.1.call-done
  956.8 31.2 %reduce-scatter.9.cloned.1.call-done = bf16[256,4096]{1,0:T(8,128)(2,1)} async-done(((bf16[1024,4096]{1,0:T(8,128)(2,1)}), bf16[256,4096]{1,0:T(8,128)(2,1)}) %reduce-scatter.9.cloned.1.call-update) | async-done | bytes 2097168 | tf_op jit(solution)/shard_map/reduce_scatter | solution.py:31
  988.0 69.4 %reduce-scatter.7.cloned.1.call-done = bf16[256,4096]{1,0:T(8,128)(2,1)} async-done(((bf16[1024,4096]{1,0:T(8,128)(2,1)}), bf16[256,4096]{1,0:T(8,128)(2,1)}) %reduce-scatter.7.cloned.1.call-update) | async-done | bytes 2097168 | tf_op jit(solution)/shard_map/reduce_scatter | solution.py:31
  1057.4 0.0 all-reduce.3.cloned.1.call-update
  1057.4 52.8 %fusion.17 = (f32[4096]{0:T(1024)S(1)}, bf16[4096,1024]{0,1:T(8,128)(2,1)}) fusion(bf16[1,4096,1024]{1,2,0:T(8,128)(2,1)} %copy.10, bf16[4096,1024]{0,1:T(8,128)(2,1)} %fusion.40, bf16[1,1024,4096]{2,1,0:T(8,128)(2,1)} %all-gather.15.cloned.1.call-done, bf16[4096,4096]{1,0:T(8,128)(2,1)} %get-tuple-element.29, f32[4096,4096]{1,0:T(8,128)} %fusion.42), kind=kOutput, calls=%fused_computation.39 | convolution fusion | flops 34485563392 | bytes 134234112 | tf_op jit(solution)/shard_map/transpose(jvp())/dot_general | solution.py:22
  1110.3 14.1 %fusion.22 = bf16[1,4096,1024]{1,2,0:T(8,128)(2,1)} fusion(bf16[4096,1024]{0,1:T(8,128)(2,1)} %fusion.23, bf16[4096,1024]{0,1:T(8,128)(2,1)} %get-tuple-element.31, bf16[1,4096,1024]{1,2,0:T(8,128)(2,1)} %copy.10, f32[4096]{0:T(1024)S(1)} %multiply_multiply_fusion, f32[4096]{0:T(1024)S(1)} %copy-done.5), kind=kLoop, calls=%fused_computation.44 | loop fusion | flops 29360128 | bytes 33587200 | tf_op jit(solution)/shard_map/broadcast_in_dim | solution.py:44
  1124.4 11.9 copy.11
  1136.3 157.3 %all-reduce.3.cloned.1.call-done = (bf16[1,256,4096]{2,1,0:T(8,128)(2,1)}, bf16[1,256,4096]{2,1,0:T(8,128)(2,1)}, bf16[1,256,4096]{2,1,0:T(8,128)(2,1)}, bf16[1,...) async-done(((bf16[1,256,4096]{2,1,0:T(8,128)(2,1)}, bf16[1,256,4096]{2,1,0:T(8,128)(2,1)}, bf16[1,256,4096]{2,1,0:T(8,128)(2,1)}, ...) | async-done | bytes 12582928 | tf_op jit(solution)/shard_map/psum | solution.py:31
  1293.6 4.6 pad_maximum_fusion.2
  1298.2 5.9 pad_maximum_fusion
  (29 shorter events, 0.1 us)
Async XLA Ops:
  7.2 64.4 %all-gather.13.cloned.1.call-start = ((), (), s32[]{:S(2)}) async-start(), calls=%async_computation.12 | async-start | bytes 10485760 | tf_op jit(solution)/shard_map/all_gather | solution.py:28
  12.0 117.8 %all-gather.15.cloned.1.call-start = ((), (), s32[]{:S(2)}) async-start(), calls=%async_computation.13 | async-start | bytes 10485760 | tf_op jit(solution)/shard_map/all_gather | solution.py:28
  16.8 185.8 %all-gather.17.cloned.1.call-start = ((), (), s32[]{:S(2)}) async-start(), calls=%async_computation.14 | async-start | bytes 10485760 | tf_op jit(solution)/shard_map/all_gather | solution.py:28
  21.5 225.1 %all-gather.23.cloned.1.call-start = ((), (), s32[]{:S(2)}) async-start(), calls=%async_computation.17 | async-start | bytes 10485760 | tf_op jit(solution)/shard_map/all_gather | solution.py:28
  22.1 282.6 %all-gather.21.cloned.1.call-start = ((), (), s32[]{:S(2)}) async-start(), calls=%async_computation.16 | async-start | bytes 10485760 | tf_op jit(solution)/shard_map/all_gather | solution.py:28
  22.7 340.6 %all-gather.19.cloned.1.call-start = ((), (), s32[]{:S(2)}) async-start(), calls=%async_computation.15 | async-start | bytes 10485760 | tf_op jit(solution)/shard_map/all_gather | solution.py:28
  23.3 933.5 %reduce-scatter.15.cloned.1.call-start = ((), (), s32[]{:S(2)}) async-start(), calls=%async_computation.10 | async-start | bytes 10485760 | tf_op jit(solution)/shard_map/reduce_scatter | solution.py:31
  40.3 0.6 copy-start
  40.9 88.9 %copy-start.2 = (f32[4096]{0:T(1024)}, f32[4096]{0:T(1024)S(1)}, u32[]{:S(2)}) copy-start(f32[4096]{0:T(1024)S(1)} %fusion.63) | copy-start | bytes 49156
  245.7 0.6 copy-start.9
  246.3 117.0 %copy-start.6 = (f32[4096]{0:T(1024)}, f32[4096]{0:T(1024)S(1)}, u32[]{:S(2)}) copy-start(f32[4096]{0:T(1024)S(1)} %fusion.64) | copy-start | bytes 49156
  490.2 52.9 %copy-start.10 = (f32[4096]{0:T(1024)S(1)}, f32[4096]{0:T(1024)}, u32[]{:S(2)}) copy-start(f32[4096]{0:T(1024)} %copy-done.9) | copy-start | bytes 49156
  490.2 52.9 %copy-start.7 = (f32[4096]{0:T(1024)S(1)}, f32[4096]{0:T(1024)}, u32[]{:S(2)}) copy-start(f32[4096]{0:T(1024)} %copy-done.6) | copy-start | bytes 49156
  599.7 357.1 %reduce-scatter.17.cloned.1.call-start = ((), (), s32[]{:S(2)}) async-start(), calls=%async_computation.11 | async-start | bytes 10485760 | tf_op jit(solution)/shard_map/reduce_scatter | solution.py:31
  652.5 304.3 %reduce-scatter.11.cloned.1.call-start = ((), (), s32[]{:S(2)}) async-start(), calls=%async_computation.8 | async-start | bytes 10485760 | tf_op jit(solution)/shard_map/reduce_scatter | solution.py:31
  652.5 83.1 %copy-start.3 = (f32[4096]{0:T(1024)S(1)}, f32[4096]{0:T(1024)}, u32[]{:S(2)}) copy-start(f32[4096]{0:T(1024)} %copy-done.2) | copy-start | bytes 49156
  735.6 46.5 %copy-start.8 = (f32[4096]{0:T(1024)S(1)}, f32[4096]{0:T(1024)}, u32[]{:S(2)}) copy-start(f32[4096]{0:T(1024)} %copy-done.6) | copy-start | bytes 49156
  782.1 174.8 %reduce-scatter.13.cloned.1.call-start = ((), (), s32[]{:S(2)}) async-start(), calls=%async_computation.9 | async-start | bytes 10485760 | tf_op jit(solution)/shard_map/reduce_scatter | solution.py:31
  828.8 42.6 %copy-start.4 = (f32[4096]{0:T(1024)S(1)}, f32[4096]{0:T(1024)}, u32[]{:S(2)}) copy-start(f32[4096]{0:T(1024)} %copy-done.2) | copy-start | bytes 49156
  828.8 159.2 %reduce-scatter.9.cloned.1.call-start = ((), (), s32[]{:S(2)}) async-start(), calls=%async_computation.7 | async-start | bytes 10485760 | tf_op jit(solution)/shard_map/reduce_scatter | solution.py:31
  871.3 186.1 %reduce-scatter.7.cloned.1.call-start = ((), (), s32[]{:S(2)}) async-start(), calls=%async_computation.6 | async-start | bytes 10485760 | tf_op jit(solution)/shard_map/reduce_scatter | solution.py:31
  913.9 379.7 %all-reduce.3.cloned.1.call-start = ((), (), s32[]{:S(2)}) async-start(), calls=%async_computation.18 | async-start | bytes 25165824 | tf_op jit(solution)/shard_map/psum | solution.py:31
  1057.4 52.9 %copy-start.1 = (f32[4096]{0:T(1024)S(1)}, f32[4096]{0:T(1024)}, u32[]{:S(2)}) copy-start(f32[4096]{0:T(1024)} %copy-done) | copy-start | bytes 49156
  1057.4 52.9 %copy-start.5 = (f32[4096]{0:T(1024)S(1)}, f32[4096]{0:T(1024)}, u32[]{:S(2)}) copy-start(f32[4096]{0:T(1024)} %copy-done.2) | copy-start | bytes 49156
Sparse Core Ops, SparseCore 0:
  12.1 59.4 all-gather.12
  73.1 56.6 all-gather.14
  131.3 56.6 all-gather.16
  190.0 56.6 all-gather.22
  248.0 56.6 all-gather.20
  306.6 56.6 all-gather.18
  599.9 66.9 reduce-scatter.14
  669.4 66.9 reduce-scatter.16
  782.2 66.9 reduce-scatter.10
  851.5 66.9 reduce-scatter.12
  921.1 66.9 reduce-scatter.8
  990.4 66.9 reduce-scatter.6
  1062.1 231.4 all-reduce.2
where the time goes:
time: 1320 us; the launch traced here: 1310 us
  matrix products  883 us (67%)
  waiting for transfers between devices  319 us (24%)
  local copies, waits for them, and re-layouts  50.7 us (4%)
  other arithmetic  43.7 us (3%)
  between operations  14.5 us (1%)
    dot_general x6, matrix products, layer(): up = jnp.dot(a, w['w_up'], preferred_element_type=jnp.float32)  317 us
    dot_general x6, matrix products, layer(): gate = jnp.dot(a, w['w_gate'], preferred_element_type=jnp.float32)  300 us
    dot_general x5, matrix products, matmul(): jnp.dot(a, w, preferred_element_type=jnp.float32).astype(jnp.bfloat16)  265 us
    psum x1, waiting for transfers between devices, summed(): lax.psum(lax.psum_scatter(term, 's', scatter_dimension=0, tiled=True), 'r')  157 us
    reduce_scatter x6, waiting for transfers between devices, summed(): lax.psum_scatter(term, 's', scatter_dimension=0, tiled=True)  101 us
    all_gather x6, waiting for transfers between devices, fetched(): lax.all_gather(w[number], 's', axis=0, tiled=True)  59.5 us
    unnamed x25, local copies, waits for them, and re-layouts  36.5 us
  transfers between devices with their start and end apart: 13, of which 8 were waited for; matrix products, arithmetic and copies ran while one was open for 55% of the time, Pallas kernels for 0%

commit v1 on v0

v1 whole, which is shorter than its diff:
```python
import jax
import jax.numpy as jnp
from jax import lax
from jax.experimental import pallas as pl
from jax.experimental.pallas import tpu as pltpu
from jax.sharding import PartitionSpec as P

F32, BF = jnp.float32, jnp.bfloat16
LIMIT = 63_000_000
NN = (((1,), (0,)), ((), ()))
NT = (((1,), (1,)), ((), ()))
TN = (((0,), (0,)), ((), ()))


def dot(a, b, dims):
    return lax.dot_general(a, b, dims, preferred_element_type=F32)


def call(body, grid, ins, outs, shapes, flops, scratch=(), name=None):
    return pl.pallas_call(
        body,
        grid=grid,
        in_specs=ins,
        out_specs=outs,
        out_shape=shapes,
        scratch_shapes=list(scratch),
        compiler_params=pltpu.CompilerParams(vmem_limit_bytes=LIMIT, dimension_semantics=("arbitrary",) * len(grid)),
        cost_estimate=pl.CostEstimate(flops=flops, bytes_accessed=100_000_000, transcendentals=0),
        name=name,
    )


def scale_of(wide):
    return lax.rsqrt(jnp.mean(wide**2, -1, keepdims=True) + 1e-6)


def sds(shape, dtype=BF):
    return jax.ShapeDtypeStruct(shape, dtype)


def dgates(dh, g, u):
    s = jax.nn.sigmoid(g)
    dh = dh.astype(F32)
    silu = g * s
    return silu, (dh * u * (s * (1 + g * (1 - s)))).astype(BF), (dh * silu).astype(BF)


def gate_up(a, wg, wu, tm=512):
    t, d = a.shape
    c, _, tn = wg.shape
    f = c * tn

    def body(a_ref, wg_ref, wu_ref, h_ref, g_ref):
        a = a_ref[...]
        g = dot(a, wg_ref[0], NN)
        g_ref[...] = g
        u = dot(a, wu_ref[0], NN)
        h_ref[...] = (g * jax.nn.sigmoid(g) * u).astype(BF)

    w = pl.BlockSpec((1, d, tn), lambda j, i: (j, 0, 0))
    o = pl.BlockSpec((tm, tn), lambda j, i: (i, j))
    return call(body, (c, t // tm), [pl.BlockSpec((tm, d), lambda j, i: (i, 0)), w, w], [o, o],
                [sds((t, f)), sds((t, f), F32)], 4 * t * d * f, name="gate_up")(a, wg, wu)


def down(hidden, wd, h, tm=512):
    t, f = hidden.shape
    nr, ns, rows, d = wd.shape

    def body(hid_ref, wd_ref, h_ref, o_ref, a_ref):
        total = jnp.zeros((tm, d), F32)
        for s in range(ns):
            w = jnp.concatenate([wd_ref[r, s] for r in range(nr)], 0)
            total += dot(hid_ref[:, s * nr * rows:(s + 1) * nr * rows], w, NN)
        y = h_ref[...] + total.astype(BF)
        o_ref[...] = y
        wide = y.astype(F32)
        a_ref[...] = (wide * scale_of(wide)).astype(BF)

    r = pl.BlockSpec((tm, d), lambda i: (i, 0))
    return call(body, (t // tm,), [pl.BlockSpec((tm, f), lambda i: (i, 0)),
                pl.BlockSpec(wd.shape, lambda i: (0, 0, 0, 0), pipeline_mode=pl.Buffered(1)), r], [r, r],
                [sds((t, d)), sds((t, d))], 2 * t * d * f, name="down")(hidden, wd, h)


def mid(a, dy, wg, wu, wd, tm=512):
    t, d = a.shape
    c, _, tn = wg.shape
    f = c * tn
    nr, ns, rows, _ = wd.shape

    def body(a_ref, dy_ref, wg_ref, wu_ref, wd_ref, h_ref, dg_ref, du_ref):
        a = a_ref[...]
        g = dot(a, wg_ref[0], NN)
        u = dot(a, wu_ref[0], NN)
        dh = dot(dy_ref[...], wd_ref[...].reshape(tn, d), NT).astype(BF)
        silu, dg_ref[...], du_ref[...] = dgates(dh, g, u)
        h_ref[...] = (silu * u).astype(BF)

    r = pl.BlockSpec((tm, d), lambda j, i: (i, 0))
    w = pl.BlockSpec((1, d, tn), lambda j, i: (j, 0, 0))
    o = pl.BlockSpec((tm, tn), lambda j, i: (i, j))
    return call(body, (c, t // tm), [r, r, w, w, pl.BlockSpec((nr, 1, rows, d), lambda j, i: (0, j, 0, 0))], [o, o, o],
                [sds((t, f))] * 3, 6 * t * d * f, name="mid")(a, dy, wg, wu, wd)


def mid_saved(a, dy, g, wu, wd, tm=512):
    t, d = dy.shape
    c, _, tn = wu.shape
    f = c * tn
    nr, ns, rows, _ = wd.shape

    def body(a_ref, dy_ref, g_ref, wu_ref, wd_ref, dg_ref, du_ref):
        u = dot(a_ref[...], wu_ref[0], NN)
        dh = dot(dy_ref[...], wd_ref[...].reshape(tn, d), NT).astype(BF)
        _, dg_ref[...], du_ref[...] = dgates(dh, g_ref[...], u)

    r = pl.BlockSpec((tm, d), lambda j, i: (i, 0))
    w = pl.BlockSpec((1, d, tn), lambda j, i: (j, 0, 0))
    o = pl.BlockSpec((tm, tn), lambda j, i: (i, j))
    return call(body, (c, t // tm), [r, r, o, w, pl.BlockSpec((nr, 1, rows, d), lambda j, i: (0, j, 0, 0))], [o, o],
                [sds((t, f))] * 2, 4 * t * d * f, name="mid_saved")(a, dy, g, wu, wd)


def by_columns(a, q, nr=4, ns=4, tn=512):
    t, d = a.shape
    f = q.shape[1]
    rows = d // (nr * ns)

    def body(a_ref, q_ref, o_ref):
        w = dot(a_ref[...], q_ref[...], TN).astype(BF)
        for s in range(ns):
            for r in range(nr):
                o_ref[r, s] = w[(s * nr + r) * rows:(s * nr + r + 1) * rows]

    return call(body, (f // tn,), [pl.BlockSpec((t, d), lambda j: (0, 0), pipeline_mode=pl.Buffered(1)),
                pl.BlockSpec((t, tn), lambda j: (0, j))], pl.BlockSpec((nr, ns, rows, tn), lambda j: (0, 0, 0, j)),
                sds((nr, ns, rows, f)), 2 * t * d * f, name="by_columns")(a, q)


def by_rows(q, dy, nr=4, ns=4, tn=512):
    t, d = dy.shape
    f = q.shape[1]
    rows = f // (nr * ns)
    each = tn // rows
    per = nr // each

    def body(dy_ref, q_ref, o_ref):
        o_ref[...] = dot(q_ref[...], dy_ref[...], TN).astype(BF).reshape(o_ref.shape)

    return call(body, (f // tn,), [pl.BlockSpec((t, d), lambda j: (0, 0), pipeline_mode=pl.Buffered(1)),
                pl.BlockSpec((t, tn), lambda j: (0, j))],
                pl.BlockSpec((each, 1, rows, d), lambda j: (j % per, j // per, 0, 0)),
                sds((nr, ns, rows, d)), 2 * t * d * f, name="by_rows")(dy, q)


def back(dg, du, wg, wu, h, dy, tm=256):
    t, f = dg.shape
    c, d, tn = wg.shape

    def body(dg_ref, du_ref, wg_ref, wu_ref, h_ref, dy_ref, o_ref):
        def through(p_ref, w_ref):
            total = jnp.zeros((tm, d), F32)
            for j in range(c):
                total += dot(p_ref[:, j * tn:(j + 1) * tn], w_ref[j], NT)
            return total.astype(BF)
        da = (through(dg_ref, wg_ref) + through(du_ref, wu_ref)).astype(F32)
        wide = h_ref[...].astype(F32)
        scale = scale_of(wide)
        by = da * scale - wide * (scale**3 * jnp.mean(da * wide, -1, keepdims=True))
        o_ref[...] = dy_ref[...] + by.astype(BF)

    r = pl.BlockSpec((tm, d), lambda i: (i, 0))
    l = pl.BlockSpec((tm, f), lambda i: (i, 0))
    w = pl.BlockSpec((c, d, tn), lambda i: (0, 0, 0), pipeline_mode=pl.Buffered(1))
    return call(body, (t // tm,), [l, l, w, w, r, r], r, sds((t, d)), 4 * t * d * f, name="back")(dg, du, wg, wu, h, dy)


def normed(h):
    wide = h.astype(F32)
    return (wide * scale_of(wide)).astype(BF)


def solution(mesh):
    nr, ns = mesh.shape["r"], mesh.shape["s"]
    everyone = ("r", "s")

    def step(x, dy, w_gate, w_up, w_down):
        x, dy = x[0], dy[0]
        me = lax.axis_index("r")
        rows, f = w_gate.shape[1:]
        deep, d = w_down.shape[1:]

        def columns(w):
            return lax.dynamic_slice_in_dim(w, me * (f // nr), f // nr, 1)

        def wide(w):
            return w.reshape(nr, ns * rows, f // nr)

        def quarter(w):
            return lax.dynamic_slice_in_dim(w, me * (deep // nr), deep // nr, 0)

        def fetch(*ws):
            return [lax.all_gather(w, everyone, axis=0, tiled=True) for w in ws]

        def fetched(number):
            g, u, w = fetch(columns(w_gate[number]), columns(w_up[number]), quarter(w_down[number]))
            return wide(g), wide(u), w.reshape(nr, ns, deep // nr, d)

        g0, u0, d0 = fetched(0)
        g1, u1, d1 = fetched(1)
        a0 = normed(x)
        hidden0, gate0 = gate_up(a0, g0, u0)
        h1, a1 = down(hidden0, d0, x)
        hidden1, dg1, du1 = mid(a1, dy, g1, u1, d1)

        def reduced(term):
            flat = term.reshape((-1,) + term.shape[3:])
            return lax.psum_scatter(flat, everyone, scatter_dimension=0, tiled=True)

        down1 = reduced(by_rows(hidden1, dy))
        dh1 = back(dg1, du1, g1, u1, h1, dy)
        gate1 = reduced(by_columns(a1, dg1))
        up1 = reduced(by_columns(a1, du1))
        dg0, du0 = mid_saved(a0, dh1, gate0, u0, d0)
        down0 = reduced(by_rows(hidden0, dh1))
        gate0_ = reduced(by_columns(a0, dg0))
        up0 = reduced(by_columns(a0, du0))
        dx = back(dg0, du0, g0, u0, x, dh1)

        def whole(first, second):
            return jnp.stack([lax.all_gather(first, "r", axis=0, tiled=True), lax.all_gather(second, "r", axis=0, tiled=True)])

        return dx[None], whole(gate0_, gate1), whole(up0, up1), whole(down0, down1)

    states, cut = P(("rep", "r", "s"), None, None), P(None, "s", None)
    return jax.shard_map(
        step,
        mesh=mesh,
        in_specs=(states, states) + (cut,) * 3,
        out_specs=(states,) + (P("rep", "s", None),) * 3,
        check_vma=False,
    )
```

time: 1320 us -> 1350 us (1.023)
  matrix products: 883 us -> 0 us
  Pallas kernels: 0 us -> 785 us
  waiting for transfers between devices: 319 us -> 494 us
  local copies, waits for them, and re-layouts: 50.7 us -> 20.1 us
  other arithmetic: 43.7 us -> 27.1 us
    dot_general x17 -> x0, matrix products: 883 us -> none  [the longest x6 317 us: layer(): up = jnp.dot(a, w['w_up'], preferred_element_type=jnp.float32)]
    pallas_call x0 -> x12, Pallas kernels: none -> 785 us  [the longest x2 172 us: back(): call(body, (t // tm,), [l, l, w, w, r, r], r, sds((t, d)), 4 * t * d * f,...]
    all_gather x6 -> x12, waiting for transfers between devices: 59.5 us -> 250 us  [the longest x6 150 us: fetch(): return [lax.all_gather(w, everyone, axis=0, tiled=True) for w in ws]]
    psum x1 -> x0, waiting for transfers between devices: 157 us -> none  [summed(): lax.psum(lax.psum_scatter(term, 's', scatter_dimension=0, tiled=True), 'r')]
    reduce_scatter x6, waiting for transfers between devices: 101 us -> 242 us  [reduced(): return lax.psum_scatter(flat, everyone, scatter_dimension=0, tiled=True)]
    unnamed x25 -> x0, local copies, waits for them, and re-layouts: 36.5 us -> none
    broadcast_in_dim x1 -> x0, other arithmetic: 14.1 us -> none  [step(): by_h[None]]
    add_any x1 -> x0, other arithmetic: 14 us -> none  [normed(): wide = h.astype(jnp.float32)]
  transfers between devices with their start and end apart: 13 -> 18, of which waited for: 8 -> 11; matrix products, arithmetic and copies ran while one was open for 55% -> 3% of each run, Pallas kernels for 0% -> 40%
where the time goes in v1:
time: 1350 us; the launch traced here: 1340 us
  Pallas kernels  785 us (58%)
  waiting for transfers between devices  494 us (37%)
  other arithmetic  27.1 us (2%)
  local copies, waits for them, and re-layouts  20.1 us (1%)
  between operations  14.6 us (1%)
    reduce_scatter x6, waiting for transfers between devices, reduced(): return lax.psum_scatter(flat, everyone, scatter_dimension=0, tiled=True)  242 us
    pallas_call x2, Pallas kernels, back(): call(body, (t // tm,), [l, l, w, w, r, r], r, sds((t, d)), 4 * t * d * f,...  172 us
    pallas_call x4, Pallas kernels, by_columns(): call(body, (f // tn,), [pl.BlockSpec((t, d), lambda j: (0, 0), pipeline_m...  168 us
    all_gather x6, waiting for transfers between devices, fetch(): return [lax.all_gather(w, everyone, axis=0, tiled=True) for w in ws]  150 us
    pallas_call x1, Pallas kernels, mid(): call(body, (c, t // tm), [r, r, w, w, pl.BlockSpec((nr, 1, rows, d), lamb...  126 us
    pallas_call x1, Pallas kernels, mid_saved(): call(body, (c, t // tm), [r, r, o, w, pl.BlockSpec((nr, 1, rows, d), lamb...  105 us
    pallas_call x1, Pallas kernels, gate_up(): call(body, (c, t // tm), [pl.BlockSpec((tm, d), lambda j, i: (i, 0)), w,...  85.4 us
    pallas_call x2, Pallas kernels, by_rows(): call(body, (f // tn,), [pl.BlockSpec((t, d), lambda j: (0, 0), pipeline_m...  84.4 us
  transfers between devices with their start and end apart: 18, of which 11 were waited for; matrix products, arithmetic and copies ran while one was open for 3% of the time, Pallas kernels for 40%

profile of v1, /device:TPU:0, one launch (start us, length us, event | category | flops | bytes accessed | tf_op | source)
XLA Modules:
  0.0 1341.3 jit_solution(13546261666913497264)
XLA Ops:
  7.2 0.0 all-gather.33.cloned.1.call-start
  7.2 3.9 fusion.3
  11.1 1.9 constant_dynamic-slice_fusion.4
  13.1 0.0 all-gather.33.cloned.1.call-update
  13.1 0.0 all-gather.31.cloned.1.call-start
  13.1 4.0 fusion.4
  17.2 0.8 constant_dynamic-slice_fusion.5
  18.0 0.0 all-gather.35.cloned.1.call-start
  18.1 4.0 fusion.2
  22.1 0.8 constant_dynamic-slice_fusion.3
  22.9 0.0 all-gather.35.cloned.1.call-update
  22.9 0.0 all-gather.37.cloned.1.call-start
  23.0 1.9 constant_dynamic-slice_fusion.2
  24.9 0.0 all-gather.37.cloned.1.call-update
  24.9 0.0 all-gather.39.cloned.1.call-start
  24.9 0.8 constant_dynamic-slice_fusion.1
  25.8 0.0 all-gather.41.cloned.1.call-start
  25.9 1.9 constant_dynamic-slice_fusion
  27.8 0.0 reduce-scatter.15.cloned.1.call-start
  27.8 5.1 fusion
  32.9 8.2 fusion.1.a_ref
  41.1 23.6 %all-gather.33.cloned.1.call-done = bf16[1,4096,1024]{2,1,0:T(8,128)(2,1)} async-done(((bf16[1,256,1024]{2,1,0:T(8,128)(2,1)}), bf16[1,4096,1024]{2,1,0:T(8,128)(2,1)}) %all-gather.33.cloned.1.call-update) | async-done | bytes 8388624 | tf_op jit(solution)/shard_map/all_gather | solution.py:204
  64.7 51.5 %all-gather.31.cloned.1.call-done = bf16[1,4096,1024]{2,1,0:T(8,128)(2,1)} async-done(((bf16[1,256,1024]{2,1,0:T(8,128)(2,1)}), bf16[1,4096,1024]{2,1,0:T(8,128)(2,1)}) %all-gather.31.cloned.1.call-update) | async-done | bytes 8388624 | tf_op jit(solution)/shard_map/all_gather | solution.py:204
  116.2 85.4 %gate_up.1 = (bf16[4096,4096]{1,0:T(8,128)(2,1)}, f32[4096,4096]{1,0:T(8,128)}) custom-call(bf16[4096,1024]{1,0:T(8,128)(2,1)} %fusion.1.a_ref, bf16[4,1024,1024]{2,1,0:T(8,128)(2,1)} %bitcast.43, bf16[4,1024,1024]{2,1,0:T(8,128)(2,1)} %bitcast.40), custom_call_target="tpu_custom_call" | custom-call | flops 68719476736 | bytes 100000000 | tf_op jit(solution)/shard_map/gate_up/pallas_call | solution.py:62
  201.6 43.5 %down.1 = (bf16[4096,1024]{1,0:T(8,128)(2,1)}, bf16[4096,1024]{1,0:T(8,128)(2,1)}) custom-call(bf16[4096,4096]{1,0:T(8,128)(2,1)} %get-tuple-element.13.hid_ref.q_ref, bf16[4,4,256,1024]{3,2,1,0:T(8,128)(2,1)} %bitcast.45, bf16[4096,1024]{1,0:T(8,128)(2,1)} %bitcast.23), custom_call_target="tpu_custom_call" | custom-call | flops 34359738368 | bytes 100000000 | tf_op jit(solution)/shard_map/down/pallas_call | solution.py:81
  245.1 24.2 %all-gather.39.cloned.1.call-done = bf16[1,4096,1024]{2,1,0:T(8,128)(2,1)} async-done(((bf16[1,256,1024]{2,1,0:T(8,128)(2,1)}), bf16[1,4096,1024]{2,1,0:T(8,128)(2,1)}) %all-gather.39.cloned.1.call-update) | async-done | bytes 8388624 | tf_op jit(solution)/shard_map/all_gather | solution.py:204
  269.3 50.8 %all-gather.41.cloned.1.call-done = bf16[1,4096,1024]{2,1,0:T(8,128)(2,1)} async-done(((bf16[1,256,1024]{2,1,0:T(8,128)(2,1)}), bf16[1,4096,1024]{2,1,0:T(8,128)(2,1)}) %all-gather.41.cloned.1.call-update) | async-done | bytes 8388624 | tf_op jit(solution)/shard_map/all_gather | solution.py:204
  320.1 126.2 %mid.1 = (bf16[4096,4096]{1,0:T(8,128)(2,1)}, bf16[4096,4096]{1,0:T(8,128)(2,1)}, bf16[4096,4096]{1,0:T(8,128)(2,1)}) custom-call(bf16[4096,1024]{1,0:T(8,128)(2,1)} %get-tuple-element.14.a_ref, bf16[4096,1024]{1,0:T(8,128)(2,1)} %bitcast.37, bf16[4,1024,1024]{2,1,0:T(8,128)(2,1)} %bitcast.47, bf16[4,1024,1024]{2,1,0:T(8,128)(2,1)} %bitcast.49, ...), custom_call_target="tpu_custom_call" | custom-call | flops 103079215104 | bytes 100000000 | tf_op jit(solution)/shard_map/mid/pallas_call | solution.py:103
  446.3 86.2 %back.2.dy_ref = bf16[4096,1024]{1,0:T(8,128)(2,1)} custom-call(bf16[4096,4096]{1,0:T(8,128)(2,1)} %get-tuple-element.15.dg_ref.q_ref, bf16[4096,4096]{1,0:T(8,128)(2,1)} %get-tuple-element.16.du_ref.q_ref, bf16[4,1024,1024]{2,1,0:T(8,128)(2,1)} %bitcast.48, bf16[4,1024,1024]{2,1,0:T(8,128)(2,1)} %bitcast.50, bf16[4096,1024]{1,0:T(8,128)(2,1)} %get-tuple-element.17.h_ref, ...), custom_call_target="tpu_custom_call" | custom-call | flops 68719476736 | bytes 100000000 | tf_op jit(solution)/shard_map/back/pallas_call | solution.py:176
  532.5 42.3 %by_rows.2 = bf16[4,4,256,1024]{3,2,1,0:T(8,128)(2,1)} custom-call(bf16[4096,1024]{1,0:T(8,128)(2,1)} %back.2.dy_ref, bf16[4096,4096]{1,0:T(8,128)(2,1)} %get-tuple-element.13.hid_ref.q_ref), custom_call_target="tpu_custom_call" | custom-call | flops 34359738368 | bytes 100000000 | tf_op jit(solution)/shard_map/by_rows/pallas_call | solution.py:151
  574.8 0.0 reduce-scatter.17.cloned.1.call-start
  574.8 42.1 %by_rows.3 = bf16[4,4,256,1024]{3,2,1,0:T(8,128)(2,1)} custom-call(bf16[4096,1024]{1,0:T(8,128)(2,1)} %bitcast.39, bf16[4096,4096]{1,0:T(8,128)(2,1)} %get-tuple-element.21.q_ref), custom_call_target="tpu_custom_call" | custom-call | flops 34359738368 | bytes 100000000 | tf_op jit(solution)/shard_map/by_rows/pallas_call | solution.py:151
  617.0 0.0 reduce-scatter.13.cloned.1.call-start
  617.0 42.1 %by_columns.7 = bf16[4,4,64,4096]{3,2,1,0:T(8,128)(2,1)} custom-call(bf16[4096,1024]{1,0:T(8,128)(2,1)} %get-tuple-element.14.a_ref, bf16[4096,4096]{1,0:T(8,128)(2,1)} %get-tuple-element.16.du_ref.q_ref), custom_call_target="tpu_custom_call" | custom-call | flops 34359738368 | bytes 100000000 | tf_op jit(solution)/shard_map/by_columns/pallas_call | solution.py:136
  659.1 0.0 reduce-scatter.11.cloned.1.call-start
  659.2 104.8 %mid_saved.1 = (bf16[4096,4096]{1,0:T(8,128)(2,1)}, bf16[4096,4096]{1,0:T(8,128)(2,1)}) custom-call(bf16[4096,1024]{1,0:T(8,128)(2,1)} %fusion.1.a_ref, bf16[4096,1024]{1,0:T(8,128)(2,1)} %back.2.dy_ref, f32[4096,4096]{1,0:T(8,128)} %get-tuple-element.18.g_ref, bf16[4,1024,1024]{2,1,0:T(8,128)(2,1)} %bitcast.41, bf16[4,4,256,1024]{3,2,1,0:T(8,128)(2,1)} %bitcast.46), custom_call_target="tpu_custom_call" | custom-call | flops 68719476736 | bytes 100000000 | tf_op jit(solution)/shard_map/mid_saved/pallas_call | solution.py:121
  764.0 42.0 %by_columns.6 = bf16[4,4,64,4096]{3,2,1,0:T(8,128)(2,1)} custom-call(bf16[4096,1024]{1,0:T(8,128)(2,1)} %fusion.1.a_ref, bf16[4096,4096]{1,0:T(8,128)(2,1)} %get-tuple-element.20.du_ref.q_ref), custom_call_target="tpu_custom_call" | custom-call | flops 34359738368 | bytes 100000000 | tf_op jit(solution)/shard_map/by_columns/pallas_call | solution.py:136
  806.1 0.0 reduce-scatter.7.cloned.1.call-start
  806.1 42.1 %by_columns.4 = bf16[4,4,64,4096]{3,2,1,0:T(8,128)(2,1)} custom-call(bf16[4096,1024]{1,0:T(8,128)(2,1)} %fusion.1.a_ref, bf16[4096,4096]{1,0:T(8,128)(2,1)} %get-tuple-element.19.dg_ref.q_ref), custom_call_target="tpu_custom_call" | custom-call | flops 34359738368 | bytes 100000000 | tf_op jit(solution)/shard_map/by_columns/pallas_call | solution.py:136
  848.2 0.0 reduce-scatter.9.cloned.1.call-start
  848.3 42.2 %by_columns.5 = bf16[4,4,64,4096]{3,2,1,0:T(8,128)(2,1)} custom-call(bf16[4096,1024]{1,0:T(8,128)(2,1)} %get-tuple-element.14.a_ref, bf16[4096,4096]{1,0:T(8,128)(2,1)} %get-tuple-element.15.dg_ref.q_ref), custom_call_target="tpu_custom_call" | custom-call | flops 34359738368 | bytes 100000000 | tf_op jit(solution)/shard_map/by_columns/pallas_call | solution.py:136
  890.5 0.0 all-gather.27.cloned.1.call-start
  890.5 0.0 reduce-scatter.15.cloned.1.call-done
  890.6 0.7 all-gather.27.cloned.1.call-update
  891.2 0.0 all-gather.29.cloned.1.call-start
  891.3 0.0 reduce-scatter.17.cloned.1.call-done
  891.3 0.5 all-gather.29.cloned.1.call-update
  891.8 0.0 all-gather.25.cloned.1.call-start
  891.9 0.0 reduce-scatter.13.cloned.1.call-done
  891.9 0.5 all-gather.25.cloned.1.call-update
  892.4 0.0 all-gather.23.cloned.1.call-start
  892.4 54.9 %reduce-scatter.11.cloned.1.call-done = bf16[64,4096]{1,0:T(8,128)(2,1)} async-done(((bf16[1024,4096]{1,0:T(8,128)(2,1)}), bf16[64,4096]{1,0:T(8,128)(2,1)}) %reduce-scatter.11.cloned.1.call-update) | async-done | bytes 524304 | tf_op jit(solution)/shard_map/reduce_scatter | solution.py:219
  947.3 0.0 all-gather.19.cloned.1.call-start
  947.4 93.2 %reduce-scatter.7.cloned.1.call-done = bf16[64,4096]{1,0:T(8,128)(2,1)} async-done(((bf16[1024,4096]{1,0:T(8,128)(2,1)}), bf16[64,4096]{1,0:T(8,128)(2,1)}) %reduce-scatter.7.cloned.1.call-update) | async-done | bytes 524304 | tf_op jit(solution)/shard_map/reduce_scatter | solution.py:219
  1040.6 0.0 all-gather.21.cloned.1.call-start
  1040.7 93.6 %reduce-scatter.9.cloned.1.call-done = bf16[64,4096]{1,0:T(8,128)(2,1)} async-done(((bf16[1024,4096]{1,0:T(8,128)(2,1)}), bf16[64,4096]{1,0:T(8,128)(2,1)}) %reduce-scatter.9.cloned.1.call-update) | async-done | bytes 524304 | tf_op jit(solution)/shard_map/reduce_scatter | solution.py:219
  1134.3 86.1 %back.3 = bf16[4096,1024]{1,0:T(8,128)(2,1)} custom-call(bf16[4096,4096]{1,0:T(8,128)(2,1)} %get-tuple-element.19.dg_ref.q_ref, bf16[4096,4096]{1,0:T(8,128)(2,1)} %get-tuple-element.20.du_ref.q_ref, bf16[4,1024,1024]{2,1,0:T(8,128)(2,1)} %bitcast.44, bf16[4,1024,1024]{2,1,0:T(8,128)(2,1)} %bitcast.42, bf16[4096,1024]{1,0:T(8,128)(2,1)} %bitcast.24, ...), custom_call_target="tpu_custom_call" | custom-call | flops 68719476736 | bytes 100000000 | tf_op jit(solution)/shard_map/back/pallas_call | solution.py:176
  1220.4 4.6 pad_maximum_fusion.2
  1225.1 6.0 all-gather.25.cloned.1.call-done
  1231.1 32.8 %all-gather.23.cloned.1.call-done = bf16[256,4096]{1,0:T(8,128)(2,1)} async-done(((bf16[64,4096]{1,0:T(8,128)(2,1)}), bf16[256,4096]{1,0:T(8,128)(2,1)}) %all-gather.23.cloned.1.call-update) | async-done | bytes 2097168 | tf_op jit(solution)/shard_map/all_gather | solution.py:232
  1263.9 4.6 pad_maximum_fusion.1
  1268.6 28.2 %all-gather.19.cloned.1.call-done = bf16[256,4096]{1,0:T(8,128)(2,1)} async-done(((bf16[64,4096]{1,0:T(8,128)(2,1)}), bf16[256,4096]{1,0:T(8,128)(2,1)}) %all-gather.19.cloned.1.call-update) | async-done | bytes 2097168 | tf_op jit(solution)/shard_map/all_gather | solution.py:232
  1296.8 32.8 %all-gather.21.cloned.1.call-done = bf16[256,4096]{1,0:T(8,128)(2,1)} async-done(((bf16[64,4096]{1,0:T(8,128)(2,1)}), bf16[256,4096]{1,0:T(8,128)(2,1)}) %all-gather.21.cloned.1.call-update) | async-done | bytes 2097168 | tf_op jit(solution)/shard_map/all_gather | solution.py:232
  1329.6 4.6 pad_maximum_fusion
  (17 shorter events, 0.2 us)
Async XLA Ops:
  7.2 57.5 %all-gather.33.cloned.1.call-start = ((), (), s32[]{:S(2)}) async-start(), calls=%async_computation.19 | async-start | bytes 8912896 | tf_op jit(solution)/shard_map/all_gather | solution.py:204
  13.1 103.1 %all-gather.31.cloned.1.call-start = ((), (), s32[]{:S(2)}) async-start(), calls=%async_computation.18 | async-start | bytes 8912896 | tf_op jit(solution)/shard_map/all_gather | solution.py:204
  18.0 183.6 %all-gather.35.cloned.1.call-start = ((), (), s32[]{:S(2)}) async-start(), calls=%async_computation.20 | async-start | bytes 8912896 | tf_op jit(solution)/shard_map/all_gather | solution.py:204
  22.9 222.2 %all-gather.37.cloned.1.call-start = ((), (), s32[]{:S(2)}) async-start(), calls=%async_computation.21 | async-start | bytes 8912896 | tf_op jit(solution)/shard_map/all_gather | solution.py:204
  24.9 244.4 %all-gather.39.cloned.1.call-start = ((), (), s32[]{:S(2)}) async-start(), calls=%async_computation.22 | async-start | bytes 8912896 | tf_op jit(solution)/shard_map/all_gather | solution.py:204
  25.8 294.2 %all-gather.41.cloned.1.call-start = ((), (), s32[]{:S(2)}) async-start(), calls=%async_computation.23 | async-start | bytes 8912896 | tf_op jit(solution)/shard_map/all_gather | solution.py:204
  27.8 862.8 %reduce-scatter.15.cloned.1.call-start = ((), (), s32[]{:S(2)}) async-start(), calls=%async_computation.14 | async-start | bytes 8912896 | tf_op jit(solution)/shard_map/reduce_scatter | solution.py:219
  574.8 316.5 %reduce-scatter.17.cloned.1.call-start = ((), (), s32[]{:S(2)}) async-start(), calls=%async_computation.16 | async-start | bytes 8912896 | tf_op jit(solution)/shard_map/reduce_scatter | solution.py:219
  617.0 274.9 %reduce-scatter.13.cloned.1.call-start = ((), (), s32[]{:S(2)}) async-start(), calls=%async_computation.12 | async-start | bytes 8912896 | tf_op jit(solution)/shard_map/reduce_scatter | solution.py:219
  659.1 288.2 %reduce-scatter.11.cloned.1.call-start = ((), (), s32[]{:S(2)}) async-start(), calls=%async_computation.10 | async-start | bytes 8912896 | tf_op jit(solution)/shard_map/reduce_scatter | solution.py:219
  806.1 234.5 %reduce-scatter.7.cloned.1.call-start = ((), (), s32[]{:S(2)}) async-start(), calls=%async_computation.6 | async-start | bytes 8912896 | tf_op jit(solution)/shard_map/reduce_scatter | solution.py:219
  848.2 286.0 %reduce-scatter.9.cloned.1.call-start = ((), (), s32[]{:S(2)}) async-start(), calls=%async_computation.8 | async-start | bytes 8912896 | tf_op jit(solution)/shard_map/reduce_scatter | solution.py:219
  890.5 329.9 %all-gather.27.cloned.1.call-start = ((), (), s32[]{:S(2)}) async-start(), calls=%async_computation.15 | async-start | bytes 2621440 | tf_op jit(solution)/shard_map/all_gather | solution.py:232
  891.2 329.2 %all-gather.29.cloned.1.call-start = ((), (), s32[]{:S(2)}) async-start(), calls=%async_computation.17 | async-start | bytes 2621440 | tf_op jit(solution)/shard_map/all_gather | solution.py:232
  891.8 339.3 %all-gather.25.cloned.1.call-start = ((), (), s32[]{:S(2)}) async-start(), calls=%async_computation.13 | async-start | bytes 2621440 | tf_op jit(solution)/shard_map/all_gather | solution.py:232
  892.4 371.6 %all-gather.23.cloned.1.call-start = ((), (), s32[]{:S(2)}) async-start(), calls=%async_computation.11 | async-start | bytes 2621440 | tf_op jit(solution)/shard_map/all_gather | solution.py:232
  947.3 349.4 %all-gather.19.cloned.1.call-start = ((), (), s32[]{:S(2)}) async-start(), calls=%async_computation.7 | async-start | bytes 2621440 | tf_op jit(solution)/shard_map/all_gather | solution.py:232
  1040.6 289.0 %all-gather.21.cloned.1.call-start = ((), (), s32[]{:S(2)}) async-start(), calls=%async_computation.9 | async-start | bytes 2621440 | tf_op jit(solution)/shard_map/all_gather | solution.py:232
Sparse Core Ops, SparseCore 0:
  13.2 51.4 all-gather.32
  67.5 48.6 all-gather.30
  118.5 48.6 all-gather.34
  169.2 48.6 all-gather.36
  220.6 48.6 all-gather.38
  271.4 48.6 all-gather.40
  574.9 92.7 reduce-scatter.14
  670.0 90.9 reduce-scatter.16
  763.2 90.9 reduce-scatter.12
  856.3 90.9 reduce-scatter.10
  949.6 90.9 reduce-scatter.6
  1043.3 90.9 reduce-scatter.8
  1136.1 29.3 all-gather.26
  1167.1 31.1 all-gather.28
  1199.9 31.1 all-gather.24
  1232.8 31.1 all-gather.22
  1265.6 31.1 all-gather.18
  1298.4 31.1 all-gather.20
